TPU v7x, 32 devices: a whole 2x2x4 slice. The times are simulated.
32 devices in a mesh: img: 2 (over x), sub: 16 (over z, y, core).
Axes of the slice: x: 2, y: 2, z: 4, core: 2. Of those that a mesh axis runs over, the one named last changes fastest.
Arguments:
- sub_images: float32 [2, 512, 4096], P(None, ('img', 'sub')), parts along dimension 1, may hold values from -6 to 6
- shift_table: int32 [4, 16, 2, 8], P(None, 'sub'), may hold values from -256 to 256
- phase_table: float32 [4, 16, 2, 8], P(None, 'sub'), may hold values from -3.140625 to 3.140625
- offset_table: int32 [4, 16, 2, 16], P(None, 'sub'), may hold values from 0 to 4
- weight_table: float32 [4, 16, 2, 4, 16], P(None, 'sub'), may hold values from -2 to 2
Outputs:
- turned_image: float32 [2, 8192, 256], P(None, ('img', 'sub')), parts along dimension 1
There are 2 independent parts, one for each index of `img`. A program takes and returns all parts, laid end to end along the dimension named above; an argument that names none is the same for every part. Nothing has to cross between parts.
All inputs are finite; a program needn't handle non-finite values.
Results may differ from a plain program's by a relative error of at most 0.0003.
Values sent between devices are 32-bit elements; how exact they have to be, the bound alone decides.
A program may use at most 64 MiB of HBM per device.

v0:
```python
import functools
import math

import jax
import jax.numpy as jnp
import numpy as np
from jax import lax
from jax.experimental import pallas as pl
from jax.experimental.pallas import tpu as pltpu
from jax.sharding import PartitionSpec as P

LANES = 128
CHUNK = 8
F32 = jnp.float32
BF16 = jnp.bfloat16


def split(values):
    high = values.astype(BF16)
    low = (values - high.astype(F32)).astype(BF16)
    return high, low


def dot(left, right):
    return jnp.dot(left, right, preferred_element_type=F32)


def times_constant(pair, constant):
    real_part, imag_part = pair
    c, s = constant.real, constant.imag
    if abs(s) < 1e-12:
        return pair if c > 0 else (-real_part, -imag_part)
    if abs(c) < 1e-12:
        return (-imag_part, real_part) if s > 0 else (imag_part, -real_part)
    if abs(abs(c) - abs(s)) < 1e-12:
        h = abs(c)
        a = real_part if c > 0 else -real_part
        b = imag_part if s > 0 else -imag_part
        e = real_part if s > 0 else -real_part
        f = imag_part if c > 0 else -imag_part
        return (a - b) * h, (e + f) * h
    return real_part * c - imag_part * s, real_part * s + imag_part * c


def butterflies(rows, direction):
    n = len(rows)
    if n == 1:
        return rows
    even = butterflies(rows[0::2], direction)
    odd = butterflies(rows[1::2], direction)
    first, second = [], []
    for k in range(n // 2):
        angle = direction * 2.0 * math.pi * k / n
        tr, ti = times_constant(odd[k], complex(math.cos(angle), math.sin(angle)))
        er, ei = even[k]
        first.append((er + tr, ei + ti))
        second.append((er - tr, ei - ti))
    return first + second


def kernel(cfg, x_hbm, shift_hbm, phase_hbm, offset_hbm, weight_hbm, wf_hbm, wi_hbm, tw_hbm, out_ref,
           x_ref, shift_ref, phase_ref, offset_ref, weight_ref, wf_ref, wi_ref, tw_ref,
           field, state, landed, raw, tables, merge, sendbuf, gathered,
           load_sem, level_send, level_recv, turn_send, turn_recv):
    n, levels, outer, beams, chunks = cfg["n"], cfg["levels"], cfg["outer"], cfg["beams"], cfg["chunks"]
    per, groups, width, rows = cfg["per"], cfg["groups"], cfg["width"], cfg["rows"]
    half = beams // 2
    size = outer // chunks
    extent = size * beams
    taps = cfg["taps"]
    total = outer * LANES
    me = lax.axis_index("sub")

    def bit(level):
        return (me // (1 << level)) % 2

    def across(mask):
        other = me
        for level in range(levels):
            if mask >> level & 1:
                other = other + (1 - 2 * bit(level)) * (1 << level)
        return other

    pairs = [(x_hbm.at[:, pl.ds(g * 8, 8)], x_ref.at[:, pl.ds(g * 8, 8)]) for g in range(beams // 8)]
    pairs += [(tw_hbm, tw_ref), (wf_hbm, wf_ref), (shift_hbm, shift_ref), (phase_hbm, phase_ref),
              (offset_hbm, offset_ref), (weight_hbm, weight_ref), (wi_hbm, wi_ref)]
    loads = [pltpu.make_async_copy(src, dst, load_sem.at[i]) for i, (src, dst) in enumerate(pairs)]
    for load in loads:
        load.start()

    barrier = pltpu.get_barrier_semaphore()
    for mask in range(1, n):
        pl.semaphore_signal(barrier, inc=1, device_id={"sub": across(mask)}, device_id_type=pl.DeviceIdType.MESH)

    later = beams // 8
    for g in range(beams // 8):
        loads[g].wait()
        if g == 0:
            loads[later].wait()
        lines = [
            tuple(x_ref[p, g * 8 : g * 8 + 8, q * LANES : (q + 1) * LANES] for p in range(2)) for q in range(outer)
        ]
        for k, (re, im) in enumerate(butterflies(lines, -1)):
            tr, ti = tw_ref[0, k : k + 1, :], tw_ref[1, k : k + 1, :]
            field[k, g * 8 : g * 8 + 8, :LANES] = re * tr + im * ti
            field[k, g * 8 : g * 8 + 8, LANES:] = im * tr - re * ti

    def prepare():
        for load in loads[later + 2 :]:
            load.wait()
        raw[...] = jnp.zeros_like(raw)
        count = 6 + 2 * taps
        for level in range(levels):
            at = level * count
            raw[at : at + 2, :half] = shift_ref[level, 0].astype(F32)
            raw[at + 2 : at + 4, :half] = phase_ref[level, 0]
            raw[at + 4 : at + 6, :beams] = offset_ref[level, 0].astype(F32)
            for child in range(2):
                raw[at + 6 + child * taps : at + 6 + (child + 1) * taps, :beams] = weight_ref[level, 0, child]
        blocks = [raw[i * LANES : (i + 1) * LANES].T for i in range(raw.shape[0] // LANES)]

        def column(level, row, extent):
            at = level * count + row
            return blocks[at // LANES][:extent, at % LANES : at % LANES + 1]

        lane = lax.broadcasted_iota(jnp.int32, (beams, LANES), 1)
        wide = lax.broadcasted_iota(jnp.int32, (beams, extent), 1)
        mask = (
            lax.broadcasted_iota(jnp.int32, (extent, extent), 0) // beams
            == lax.broadcasted_iota(jnp.int32, (extent, extent), 1) // beams
        )
        slot = wide % beams
        second = slot >= half
        place = (slot % half).astype(F32)
        for level in range(levels):
            shift = jnp.concatenate([column(level, child, half) for child in range(2)], axis=0).astype(jnp.int32)
            phase = jnp.concatenate([column(level, 2 + child, half) for child in range(2)], axis=0)
            signed = jnp.where(lane >= LANES // 2, lane - LANES, lane) * outer
            unit = 2.0 * math.pi / (4 * total)
            coarse = phase - ((signed * shift) & (4 * total - 1)).astype(F32) * unit
            fine = ((lane * shift) & (4 * total - 1)).astype(F32) * (-unit)
            tables[level, 0] = jnp.cos(coarse)
            tables[level, 1] = jnp.sin(coarse)
            tables[level, 2] = jnp.cos(fine)
            tables[level, 3] = jnp.sin(fine)
            first = jnp.where(second, column(level, 5, beams), column(level, 4, beams))
            block = jnp.zeros((beams, extent), F32)
            for t in range(taps):
                weight = jnp.where(second, column(level, 6 + taps + t, beams), column(level, 6 + t, beams))
                block = block + jnp.where(place == first + t, weight, 0.0)
            tiled = jnp.concatenate([block] * size, axis=0)
            high, low = split(jnp.where(mask, tiled, 0.0))
            merge[level, 0] = high
            merge[level, 1] = low

    def level_copy(level, c):
        return pltpu.make_async_remote_copy(
            src_ref=state.at[level, c, 1 - bit(level)],
            dst_ref=landed.at[level, c],
            send_sem=level_send.at[level, c],
            recv_sem=level_recv.at[level, c],
            device_id={"sub": across(1 << level)},
            device_id_type=pl.DeviceIdType.MESH,
        )

    def publish(level, c, values):
        values = values.reshape(size, 2, half, 2 * LANES)
        for h in range(2):
            state[level, c, h] = values[:, h]
        level_copy(level, c).start()

    def transformed(values, w_ref):
        high, low = split(values)
        return dot(high, w_ref[0]) + dot(low, w_ref[0]) + dot(high, w_ref[1])

    loads[later + 1].wait()
    for c in range(chunks):
        values = transformed(field[c * size : (c + 1) * size].reshape(size * beams, 2 * LANES), wf_ref)
        if c == 0:
            pl.semaphore_wait(barrier, n - 1)
        publish(0, c, values)
    prepare()

    def stage(level, c):
        fr, fi = [], []
        cr, ci = tables[level, 0], tables[level, 1]
        sr, si = tables[level, 2], tables[level, 3]
        for k in range(c * size, (c + 1) * size):
            ar, ai = sr[:, k : k + 1], si[:, k : k + 1]
            fr.append(cr * ar - ci * ai)
            fi.append(cr * ai + ci * ar)
        fr, fi = jnp.stack(fr), jnp.stack(fi)
        level_copy(level, c).wait_recv()
        kept = state[level, c, bit(level)]
        both = jnp.concatenate([kept, landed[level, c]], axis=1)
        zr, zi = both[..., :LANES], both[..., LANES:]
        turned = jnp.concatenate([zr * fr - zi * fi, zr * fi + zi * fr], axis=-1)
        high, low = split(turned.reshape(size * beams, 2 * LANES))
        values = dot(merge[level, 0], high) + dot(merge[level, 0], low) + dot(merge[level, 1], high)
        if level + 1 < levels:
            publish(level + 1, c, values)
            return
        back = transformed(values, wi_ref).reshape(size, beams, 2 * LANES)
        for k in range(size):
            at = c * size + k
            tr, ti = tw_ref[0, at : at + 1, :], tw_ref[1, at : at + 1, :]
            re, im = back[k, :, :LANES], back[k, :, LANES:]
            field[at, :, :LANES] = re * tr - im * ti
            field[at, :, LANES:] = im * tr + re * ti

    def turn_order(at):
        level, c = at
        return (level + c if level + 1 < levels else level + 2 + 2 * c, level)

    for level, c in sorted(((a, b) for a in range(levels) for b in range(chunks)), key=turn_order):
        stage(level, c)

    for g in range(beams // 8):
        at = slice(g * 8, g * 8 + 8)
        lines = [(field[k, at, :LANES], field[k, at, LANES:]) for k in range(outer)]
        for q, pair in enumerate(butterflies(lines, 1)):
            for p in range(2):
                if groups == 1:
                    sendbuf[q // per, q % per, p, at] = pair[p]
                else:
                    field[q, at, p * LANES : (p + 1) * LANES] = pair[p]
    if groups > 1:
        for q in range(outer):
            for p in range(2):
                line = field[q, :, p * LANES : (p + 1) * LANES]
                for g in range(groups):
                    parts = [line[s * rows : (s + 1) * rows, g * width : (g + 1) * width] for s in range(groups)]
                    sendbuf[q * groups + g, 0, p] = jnp.concatenate(parts, axis=1)

    def turn_copy(mask):
        return pltpu.make_async_remote_copy(
            src_ref=sendbuf.at[across(mask)],
            dst_ref=gathered.at[me],
            send_sem=turn_send.at[mask],
            recv_sem=turn_recv.at[mask],
            device_id={"sub": across(mask)},
            device_id_type=pl.DeviceIdType.MESH,
        )

    for mask in range(n - 1, 0, -1):
        turn_copy(mask).start()
    gathered[me] = sendbuf[me]
    for level in range(levels):
        for c in range(chunks):
            level_copy(level, c).wait_send()
    for mask in range(1, n):
        pltpu.make_async_remote_copy(
            src_ref=sendbuf.at[across(mask)],
            dst_ref=gathered.at[across(mask)],
            send_sem=turn_send.at[mask],
            recv_sem=turn_recv.at[mask],
            device_id={"sub": across(mask)},
            device_id_type=pl.DeviceIdType.MESH,
        ).wait_recv()
    for p in range(2):
        for r in range(per):
            if groups == 1:
                block = gathered[:, r, p].reshape(n * beams, LANES)
                out_ref[p, r * LANES : (r + 1) * LANES, :] = block.T
            else:
                out_ref[:, r, p] = gathered[:, r, p]
    for mask in range(1, n):
        turn_copy(mask).wait_send()


def real_form(length, direction, factor):
    index = np.arange(length)
    turns = (index[:, None] * index[None, :] % length) * (direction * 2.0 * np.pi / length)
    c, s = np.cos(turns) * factor, np.sin(turns) * factor
    full = np.block([[c, s], [-s, c]]).astype(np.float32)
    high = np.asarray(full, dtype=jnp.bfloat16)
    low = np.asarray(full - high.astype(np.float32), dtype=jnp.bfloat16)
    return np.stack([high, low])


def body(n, sub_images, shift_table, phase_table, offset_table, weight_table):
    beams, bins = sub_images.shape[1], sub_images.shape[2]
    levels, taps = shift_table.shape[0], weight_table.shape[3]
    outer = bins // LANES
    share = bins // n
    per = max(1, share // LANES)
    groups = max(1, LANES // share)
    size = CHUNK
    chunks = outer // size
    rows = beams // groups
    cfg = dict(n=n, levels=levels, outer=outer, beams=beams, chunks=chunks, per=per, groups=groups,
               width=min(share, LANES), rows=rows, taps=taps)
    turns = np.arange(outer)[:, None] * np.arange(LANES)[None, :] * (2.0 * np.pi / bins)
    twiddle = np.stack([np.cos(turns), np.sin(turns)]).astype(np.float32)
    final = (2, per * LANES, n * beams) if groups == 1 else (n, per, 2, rows, LANES)
    vmem = pl.BlockSpec(memory_space=pltpu.VMEM)
    operands = (
        sub_images, shift_table, phase_table, offset_table, weight_table, jnp.asarray(real_form(LANES, -1, 1.0)),
        jnp.asarray(real_form(LANES, 1, 1.0 / bins)), jnp.asarray(twiddle),
    )
    result = pl.pallas_call(
        functools.partial(kernel, cfg),
        name="merges",
        out_shape=jax.ShapeDtypeStruct(final, F32),
        in_specs=[pl.BlockSpec(memory_space=pltpu.HBM)] * 8,
        out_specs=vmem,
        scratch_shapes=[
            *[pltpu.VMEM(a.shape, a.dtype) for a in operands],
            pltpu.VMEM((outer, beams, 2 * LANES), F32),
            pltpu.VMEM((levels, chunks, 2, size, beams // 2, 2 * LANES), F32),
            pltpu.VMEM((levels, chunks, size, beams // 2, 2 * LANES), F32),
            pltpu.VMEM((-(-levels * (6 + 2 * taps) // LANES) * LANES, LANES), F32),
            pltpu.VMEM((levels, 4, beams, LANES), F32),
            pltpu.VMEM((levels, 2, size * beams, size * beams), BF16),
            pltpu.VMEM((n, per, 2, rows, LANES), F32),
            pltpu.VMEM((n, per, 2, rows, LANES), F32),
            pltpu.SemaphoreType.DMA((beams // 8 + 7,)),
            pltpu.SemaphoreType.DMA((levels, chunks)),
            pltpu.SemaphoreType.DMA((levels, chunks)),
            pltpu.SemaphoreType.DMA((n,)),
            pltpu.SemaphoreType.DMA((n,)),
        ],
        compiler_params=pltpu.CompilerParams(
            collective_id=0, has_side_effects=True, vmem_limit_bytes=66400000
        ),
    )(*operands)
    if groups == 1:
        return result
    pieces = result.reshape(n, 2, rows, groups, share)
    return pieces.transpose(1, 4, 0, 3, 2).reshape(2, share, n * beams)


def solution(mesh):
    placed = (
        P(None, ("img", "sub"), None),
        P(None, "sub", None, None),
        P(None, "sub", None, None),
        P(None, "sub", None, None),
        P(None, "sub", None, None, None),
    )
    return jax.shard_map(
        functools.partial(body, mesh.shape["sub"]),
        mesh=mesh, in_specs=placed, out_specs=P(None, ("img", "sub"), None), check_vma=False,
    )
```

profile of v0, /device:TPU:0, one launch (start us, length us, event | category | flops | bytes accessed | tf_op | source)
XLA Modules:
  0.0 40.9 jit_solution(8596151952821660364)
XLA Ops:
  0.0 39.1 %merges.1 = f32[2,256,256]{2,1,0:T(8,128)} custom-call(f32[2,16,4096]{2,1,0:T(8,128)} %x_hbm.1, s32[4,1,2,8]{3,2,1,0:T(2,128)} %shift_hbm.1, f32[4,1,2,8]{3,2,1,0:T(2,128)} %phase_hbm.1, s32[4,1,2,16]{3,2,1,0:T(2,128)} %offset_hbm.1, f32[4,1,2,4,16]{4,3,2,1,0:T(4,128)} %weight_hbm.1, bf16[2,256,256]{2,1,0:T(8,128)(2,1)} %constant.6.clone.wf_hbm, ...), custom_call_target="tpu_custom_call" | custom-call | tf_op jit(solution)/shard_map/merges/pallas_call | solution.py:301
  39.1 1.9 %copy.10 = f32[2,256,256]{2,1,0:T(8,128)} copy(f32[2,256,256]{2,1,0:T(8,128)} %merges.1) | data formatting | bytes 1048576
where the time goes:
time: 41.1 us; the launch traced here: 40.9 us
  Pallas kernels  39.1 us (95%)
  local copies, waits for them, and re-layouts  1.87 us (5%)
    pallas_call x1, Pallas kernels, body(): pl.pallas_call(functools.partial(kernel, cfg), name='merges', out_shape=j...  39.1 us
    unnamed x1, local copies, waits for them, and re-layouts  1.87 us

commit v1 on v0

--- a/solution.py
+++ b/solution.py
@@ -58,10 +58,11 @@
     return first + second
 
 
-def kernel(cfg, x_hbm, shift_hbm, phase_hbm, offset_hbm, weight_hbm, wf_hbm, wi_hbm, tw_hbm, out_ref,
-           x_ref, shift_ref, phase_ref, offset_ref, weight_ref, wf_ref, wi_ref, tw_ref,
-           field, state, landed, raw, tables, merge, sendbuf, gathered,
-           load_sem, level_send, level_recv, turn_send, turn_recv):
+def kernel(cfg, x_hbm, shift_hbm, phase_hbm, offset_hbm, weight_hbm, wf_hbm, wi_hbm, tw_hbm, *refs):
+    outs, refs = refs[: cfg["outs"]], refs[cfg["outs"] :]
+    (x_ref, shift_ref, phase_ref, offset_ref, weight_ref, wf_ref, wi_ref, tw_ref,
+     field, state, landed, raw, tables, merge, sendbuf, gathered, card, cards, last,
+     load_sem, level_send, level_recv, turn_send, turn_recv, card_send, card_recv) = refs
     n, levels, outer, beams, chunks = cfg["n"], cfg["levels"], cfg["outer"], cfg["beams"], cfg["chunks"]
     per, groups, width, rows = cfg["per"], cfg["groups"], cfg["width"], cfg["rows"]
     half = beams // 2
@@ -69,6 +70,7 @@
     extent = size * beams
     taps = cfg["taps"]
     total = outer * LANES
+    final = levels - 1
     me = lax.axis_index("sub")
 
     def bit(level):
@@ -105,9 +107,38 @@
             field[k, g * 8 : g * 8 + 8, :LANES] = re * tr + im * ti
             field[k, g * 8 : g * 8 + 8, LANES:] = im * tr - re * ti
 
+    def card_copy(v):
+        there = (me + v) % n
+        return pltpu.make_async_remote_copy(
+            src_ref=card, dst_ref=cards.at[me], send_sem=card_send.at[v], recv_sem=card_recv.at[v],
+            device_id={"sub": there}, device_id_type=pl.DeviceIdType.MESH,
+        )
+
+    def card_arrival(v):
+        return pltpu.make_async_remote_copy(
+            src_ref=card, dst_ref=cards.at[(me + n - v) % n], send_sem=card_send.at[v], recv_sem=card_recv.at[v],
+            device_id={"sub": (me + n - v) % n}, device_id_type=pl.DeviceIdType.MESH,
+        )
+
+    def write_card():
+        for load in loads[later + 2 : later + 6]:
+            load.wait()
+        place = lax.broadcasted_iota(jnp.int32, (half, beams), 0)
+        blocks = []
+        for child in range(2):
+            first = offset_ref[final, 0, child : child + 1, :]
+            block = jnp.zeros((half, beams), F32)
+            for t in range(taps):
+                block = block + jnp.where(place == first + t, weight_ref[final, 0, child, t : t + 1, :], 0.0)
+            blocks.append(block)
+        eye = lax.broadcasted_iota(jnp.int32, (half, half), 0) == lax.broadcasted_iota(jnp.int32, (half, half), 1)
+        for row in (shift_ref[final, 0, 1:2, :].astype(F32), phase_ref[final, 0, 1:2, :]):
+            blocks.append(jnp.sum(jnp.where(eye, row, 0.0), axis=1, keepdims=True))
+        blocks.append(jnp.zeros((half, LANES - 2 * beams - 2), F32))
+        card[...] = jnp.concatenate(blocks, axis=1)
+
     def prepare():
-        for load in loads[later + 2 :]:
-            load.wait()
+        loads[later + 6].wait()
         raw[...] = jnp.zeros_like(raw)
         count = 6 + 2 * taps
         for level in range(levels):
@@ -132,9 +163,19 @@
         slot = wide % beams
         second = slot >= half
         place = (slot % half).astype(F32)
+        card_arrival(n // 2).wait_recv()
+        other = cards[(me + n // 2) % n]
         for level in range(levels):
-            shift = jnp.concatenate([column(level, child, half) for child in range(2)], axis=0).astype(jnp.int32)
-            phase = jnp.concatenate([column(level, 2 + child, half) for child in range(2)], axis=0)
+            shifts = [column(level, child, half) for child in range(2)]
+            phases = [column(level, 2 + child, half) for child in range(2)]
+            if level == final:
+                own_first = bit(final) == 0
+                a, b = shifts[0], other[:, 2 * beams : 2 * beams + 1]
+                shifts = [jnp.where(own_first, a, b), jnp.where(own_first, b, a)]
+                a, b = phases[0], other[:, 2 * beams + 1 : 2 * beams + 2]
+                phases = [jnp.where(own_first, a, b), jnp.where(own_first, b, a)]
+            shift = jnp.concatenate(shifts, axis=0).astype(jnp.int32)
+            phase = jnp.concatenate(phases, axis=0)
             signed = jnp.where(lane >= LANES // 2, lane - LANES, lane) * outer
             unit = 2.0 * math.pi / (4 * total)
             coarse = phase - ((signed * shift) & (4 * total - 1)).astype(F32) * unit
@@ -143,6 +184,8 @@
             tables[level, 1] = jnp.sin(coarse)
             tables[level, 2] = jnp.cos(fine)
             tables[level, 3] = jnp.sin(fine)
+            if level == final:
+                continue
             first = jnp.where(second, column(level, 5, beams), column(level, 4, beams))
             block = jnp.zeros((beams, extent), F32)
             for t in range(taps):
@@ -177,11 +220,14 @@
     for c in range(chunks):
         values = transformed(field[c * size : (c + 1) * size].reshape(size * beams, 2 * LANES), wf_ref)
         if c == 0:
+            write_card()
             pl.semaphore_wait(barrier, n - 1)
         publish(0, c, values)
+    for v in range(1, n):
+        card_copy(v).start()
     prepare()
 
-    def stage(level, c):
+    def turned(level, c, both):
         fr, fi = [], []
         cr, ci = tables[level, 0], tables[level, 1]
         sr, si = tables[level, 2], tables[level, 3]
@@ -190,16 +236,19 @@
             fr.append(cr * ar - ci * ai)
             fi.append(cr * ai + ci * ar)
         fr, fi = jnp.stack(fr), jnp.stack(fi)
+        zr, zi = both[..., :LANES], both[..., LANES:]
+        return jnp.concatenate([zr * fr - zi * fi, zr * fi + zi * fr], axis=-1).reshape(size * beams, 2 * LANES)
+
+    def stage(level, c):
         level_copy(level, c).wait_recv()
         kept = state[level, c, bit(level)]
         both = jnp.concatenate([kept, landed[level, c]], axis=1)
-        zr, zi = both[..., :LANES], both[..., LANES:]
-        turned = jnp.concatenate([zr * fr - zi * fi, zr * fi + zi * fr], axis=-1)
-        high, low = split(turned.reshape(size * beams, 2 * LANES))
+        high, low = split(turned(level, c, both))
         values = dot(merge[level, 0], high) + dot(merge[level, 0], low) + dot(merge[level, 1], high)
-        if level + 1 < levels:
+        if level + 1 < final:
             publish(level + 1, c, values)
             return
+        values = turned(final, c, values.reshape(size, beams, 2 * LANES))
         back = transformed(values, wi_ref).reshape(size, beams, 2 * LANES)
         for k in range(size):
             at = c * size + k
@@ -210,9 +259,9 @@
 
     def turn_order(at):
         level, c = at
-        return (level + c if level + 1 < levels else level + 2 + 2 * c, level)
-
-    for level, c in sorted(((a, b) for a in range(levels) for b in range(chunks)), key=turn_order):
+        return (2.1 * level + c if level else c - chunks, level)
+
+    for level, c in sorted(((a, b) for a in range(final) for b in range(chunks)), key=turn_order):
         stage(level, c)
 
     for g in range(beams // 8):
@@ -232,40 +281,68 @@
                     parts = [line[s * rows : (s + 1) * rows, g * width : (g + 1) * width] for s in range(groups)]
                     sendbuf[q * groups + g, 0, p] = jnp.concatenate(parts, axis=1)
 
-    def turn_copy(mask):
+    def turn_copy(v):
+        there = (me + v) % n
         return pltpu.make_async_remote_copy(
-            src_ref=sendbuf.at[across(mask)],
-            dst_ref=gathered.at[me],
-            send_sem=turn_send.at[mask],
-            recv_sem=turn_recv.at[mask],
-            device_id={"sub": across(mask)},
-            device_id_type=pl.DeviceIdType.MESH,
-        )
-
-    for mask in range(n - 1, 0, -1):
-        turn_copy(mask).start()
+            src_ref=sendbuf.at[there], dst_ref=gathered.at[me], send_sem=turn_send.at[v], recv_sem=turn_recv.at[v],
+            device_id={"sub": there}, device_id_type=pl.DeviceIdType.MESH,
+        )
+
+    def turn_arrival(v):
+        here = (me + n - v) % n
+        return pltpu.make_async_remote_copy(
+            src_ref=sendbuf.at[here], dst_ref=gathered.at[here], send_sem=turn_send.at[v], recv_sem=turn_recv.at[v],
+            device_id={"sub": here}, device_id_type=pl.DeviceIdType.MESH,
+        )
+
+    for v in range(1, n):
+        turn_copy(v).start()
     gathered[me] = sendbuf[me]
-    for level in range(levels):
+    cards[me] = card[...]
+    for v in range(1, n):
+        if v != n // 2:
+            card_arrival(v).wait_recv()
+    families = n // 16
+    if groups == 1:
+        lane = lax.broadcasted_iota(jnp.int32, (half, LANES), 1)
+        for h in range(2):
+            for g in range(families):
+                tiles = []
+                for side in range(2):
+                    for f in range(8):
+                        values = cards[h * (n // 2) + g * 8 + f]
+                        child = side ^ h
+                        moved = pltpu.roll(values, (f - child) * beams % LANES, 1)
+                        tiles.append(jnp.where((lane >= f * beams) & (lane < (f + 1) * beams), moved, 0.0))
+                high, low = split(jnp.concatenate(tiles, axis=0))
+                last[h, g, 0] = high
+                last[h, g, 1] = low
+    for level in range(final):
         for c in range(chunks):
             level_copy(level, c).wait_send()
-    for mask in range(1, n):
-        pltpu.make_async_remote_copy(
-            src_ref=sendbuf.at[across(mask)],
-            dst_ref=gathered.at[across(mask)],
-            send_sem=turn_send.at[mask],
-            recv_sem=turn_recv.at[mask],
-            device_id={"sub": across(mask)},
-            device_id_type=pl.DeviceIdType.MESH,
-        ).wait_recv()
-    for p in range(2):
+    for v in range(1, n):
+        card_copy(v).wait_send()
+    for v in range(1, n):
+        turn_arrival(v).wait_recv()
+    if groups == 1:
         for r in range(per):
-            if groups == 1:
-                block = gathered[:, r, p].reshape(n * beams, LANES)
-                out_ref[p, r * LANES : (r + 1) * LANES, :] = block.T
-            else:
-                out_ref[:, r, p] = gathered[:, r, p]
-    for mask in range(1, n):
-        turn_copy(mask).wait_send()
+            for p in range(2):
+                for h in range(2):
+                    for g in range(families):
+                        sides = [
+                            gathered[at : at + 8, r, p, h * half : (h + 1) * half].reshape(LANES // 2, LANES)
+                            for at in (g * 8, n // 2 + g * 8)
+                        ]
+                        high, low = split(jnp.concatenate(sides, axis=0).T)
+                        value = dot(high, last[h, g, 0]) + dot(low, last[h, g, 0]) + dot(high, last[h, g, 1])
+                        at = (h * families + g) * LANES
+                        outs[0][p, r * LANES : (r + 1) * LANES, at : at + LANES] = value
+    else:
+        for p in range(2):
+            outs[0][:, :, p] = gathered[:, :, p]
+        outs[1][...] = cards[...]
+    for v in range(1, n):
+        turn_copy(v).wait_send()
 
 
 def real_form(length, direction, factor):
@@ -292,7 +369,9 @@
                width=min(share, LANES), rows=rows, taps=taps)
     turns = np.arange(outer)[:, None] * np.arange(LANES)[None, :] * (2.0 * np.pi / bins)
     twiddle = np.stack([np.cos(turns), np.sin(turns)]).astype(np.float32)
-    final = (2, per * LANES, n * beams) if groups == 1 else (n, per, 2, rows, LANES)
+    half = beams // 2
+    shapes = [(2, per * LANES, n * beams)] if groups == 1 else [(n, per, 2, rows, LANES), (n, half, LANES)]
+    cfg["outs"] = len(shapes)
     vmem = pl.BlockSpec(memory_space=pltpu.VMEM)
     operands = (
         sub_images, shift_table, phase_table, offset_table, weight_table, jnp.asarray(real_form(LANES, -1, 1.0)),
@@ -301,33 +380,45 @@
     result = pl.pallas_call(
         functools.partial(kernel, cfg),
         name="merges",
-        out_shape=jax.ShapeDtypeStruct(final, F32),
+        out_shape=[jax.ShapeDtypeStruct(shape, F32) for shape in shapes],
         in_specs=[pl.BlockSpec(memory_space=pltpu.HBM)] * 8,
-        out_specs=vmem,
+        out_specs=[vmem] * len(shapes),
         scratch_shapes=[
             *[pltpu.VMEM(a.shape, a.dtype) for a in operands],
             pltpu.VMEM((outer, beams, 2 * LANES), F32),
-            pltpu.VMEM((levels, chunks, 2, size, beams // 2, 2 * LANES), F32),
-            pltpu.VMEM((levels, chunks, size, beams // 2, 2 * LANES), F32),
+            pltpu.VMEM((levels - 1, chunks, 2, size, beams // 2, 2 * LANES), F32),
+            pltpu.VMEM((levels - 1, chunks, size, beams // 2, 2 * LANES), F32),
             pltpu.VMEM((-(-levels * (6 + 2 * taps) // LANES) * LANES, LANES), F32),
             pltpu.VMEM((levels, 4, beams, LANES), F32),
-            pltpu.VMEM((levels, 2, size * beams, size * beams), BF16),
+            pltpu.VMEM((levels - 1, 2, size * beams, size * beams), BF16),
             pltpu.VMEM((n, per, 2, rows, LANES), F32),
             pltpu.VMEM((n, per, 2, rows, LANES), F32),
+            pltpu.VMEM((half, LANES), F32),
+            pltpu.VMEM((n, half, LANES), F32),
+            pltpu.VMEM((2, n // 16, 2, LANES, LANES), BF16),
             pltpu.SemaphoreType.DMA((beams // 8 + 7,)),
-            pltpu.SemaphoreType.DMA((levels, chunks)),
-            pltpu.SemaphoreType.DMA((levels, chunks)),
-            pltpu.SemaphoreType.DMA((n,)),
-            pltpu.SemaphoreType.DMA((n,)),
+            pltpu.SemaphoreType.DMA((levels - 1, chunks)),
+            pltpu.SemaphoreType.DMA((levels - 1, chunks)),
+            *[pltpu.SemaphoreType.DMA((n,))] * 4,
         ],
         compiler_params=pltpu.CompilerParams(
             collective_id=0, has_side_effects=True, vmem_limit_bytes=66400000
         ),
     )(*operands)
     if groups == 1:
-        return result
-    pieces = result.reshape(n, 2, rows, groups, share)
-    return pieces.transpose(1, 4, 0, 3, 2).reshape(2, share, n * beams)
+        return result[0]
+    pieces = result[0].reshape(n, 2, rows, groups, share).transpose(1, 4, 0, 3, 2)
+    pieces = pieces.reshape(2, share, 2, n // 2, 2, half)
+    blocks = result[1][:, :, : 2 * beams].reshape(2, n // 2, half, 2, beams)
+    sums = []
+    for h in range(2):
+        total = 0.0
+        for child in range(2):
+            total = total + jnp.einsum(
+                "pqim,imj->pqij", pieces[:, :, h ^ child, :, h], blocks[h, :, :, child], precision=lax.Precision.HIGHEST
+            )
+        sums.append(total)
+    return jnp.stack(sums, axis=2).reshape(2, share, n * beams)
 
 
 def solution(mesh):

time: 41.1 us -> 35.8 us (0.87)
  the two profiles are of different devices: /device:TPU:0 before, /device:TPU:11 now
where the time goes in v1:
time: 35.8 us; the launch traced here: 35.6 us
  Pallas kernels  33.7 us (94%)
  local copies, waits for them, and re-layouts  1.87 us (5%)
    pallas_call x1, Pallas kernels, body(): pl.pallas_call(functools.partial(kernel, cfg), name='merges', out_shape=[...  33.7 us
    unnamed x1, local copies, waits for them, and re-layouts  1.87 us

profile of v1, /device:TPU:11, one launch (start us, length us, event | category | flops | bytes accessed | tf_op | source)
XLA Modules:
  0.0 35.6 jit_solution(3167695414072823515)
XLA Ops:
  0.0 33.7 %merges.1 = f32[2,256,256]{2,1,0:T(8,128)} custom-call(f32[2,16,4096]{2,1,0:T(8,128)} %x_hbm.1, s32[4,1,2,8]{3,2,1,0:T(2,128)} %shift_hbm.1, f32[4,1,2,8]{3,2,1,0:T(2,128)} %phase_hbm.1, s32[4,1,2,16]{3,2,1,0:T(2,128)} %offset_hbm.1, f32[4,1,2,4,16]{4,3,2,1,0:T(4,128)} %weight_hbm.1, bf16[2,256,256]{2,1,0:T(8,128)(2,1)} %constant.6.clone.wf_hbm, ...), custom_call_target="tpu_custom_call" | custom-call | tf_op jit(solution)/shard_map/merges/pallas_call | solution.py:380
  33.7 1.9 %copy.10 = f32[2,256,256]{2,1,0:T(8,128)} copy(f32[2,256,256]{2,1,0:T(8,128)} %merges.1) | data formatting | bytes 1048576

commit v2 on v1

--- a/solution.py
+++ b/solution.py
@@ -10,7 +10,8 @@
 from jax.sharding import PartitionSpec as P
 
 LANES = 128
-CHUNK = 8
+CHUNKS = (1, 1, 2, 2, 1, 1)
+VMEM = 67043328 - (3 << 16)
 F32 = jnp.float32
 BF16 = jnp.bfloat16
 
@@ -59,15 +60,17 @@
 
 
 def kernel(cfg, x_hbm, shift_hbm, phase_hbm, offset_hbm, weight_hbm, wf_hbm, wi_hbm, tw_hbm, *refs):
-    outs, refs = refs[: cfg["outs"]], refs[cfg["outs"] :]
+    gathered, more, refs = refs[0], refs[1], refs[2:]
     (x_ref, shift_ref, phase_ref, offset_ref, weight_ref, wf_ref, wi_ref, tw_ref,
-     field, state, landed, raw, tables, merge, sendbuf, gathered, card, cards, last,
+     field, state, landed, raw, columns, tables, merge, sendbuf, card, cards,
      load_sem, level_send, level_recv, turn_send, turn_recv, card_send, card_recv) = refs
-    n, levels, outer, beams, chunks = cfg["n"], cfg["levels"], cfg["outer"], cfg["beams"], cfg["chunks"]
+    n, levels, outer, beams, sizes = cfg["n"], cfg["levels"], cfg["outer"], cfg["beams"], cfg["sizes"]
     per, groups, width, rows = cfg["per"], cfg["groups"], cfg["width"], cfg["rows"]
     half = beams // 2
-    size = outer // chunks
-    extent = size * beams
+    chunks = len(sizes)
+    starts = [sum(sizes[:c]) for c in range(chunks)]
+    most = max(sizes)
+    extent = most * beams
     taps = cfg["taps"]
     total = outer * LANES
     final = levels - 1
@@ -137,10 +140,10 @@
         blocks.append(jnp.zeros((half, LANES - 2 * beams - 2), F32))
         card[...] = jnp.concatenate(blocks, axis=1)
 
-    def prepare():
-        loads[later + 6].wait()
+    count = 6 + 2 * taps
+
+    def write_columns():
         raw[...] = jnp.zeros_like(raw)
-        count = 6 + 2 * taps
         for level in range(levels):
             at = level * count
             raw[at : at + 2, :half] = shift_ref[level, 0].astype(F32)
@@ -148,13 +151,37 @@
             raw[at + 4 : at + 6, :beams] = offset_ref[level, 0].astype(F32)
             for child in range(2):
                 raw[at + 6 + child * taps : at + 6 + (child + 1) * taps, :beams] = weight_ref[level, 0, child]
-        blocks = [raw[i * LANES : (i + 1) * LANES].T for i in range(raw.shape[0] // LANES)]
-
-        def column(level, row, extent):
+        for i in range(raw.shape[0] // LANES):
+            columns[i] = raw[i * LANES : (i + 1) * LANES].T
+
+    def prepare(level):
+        def column(row, extent):
             at = level * count + row
-            return blocks[at // LANES][:extent, at % LANES : at % LANES + 1]
+            return columns[at // LANES, :extent, at % LANES : at % LANES + 1]
 
         lane = lax.broadcasted_iota(jnp.int32, (beams, LANES), 1)
+        shifts = [column(child, half) for child in range(2)]
+        phases = [column(2 + child, half) for child in range(2)]
+        if level == final:
+            card_arrival(n // 2).wait_recv()
+            other = cards[(me + n // 2) % n]
+            own_first = bit(final) == 0
+            a, b = shifts[0], other[:, 2 * beams : 2 * beams + 1]
+            shifts = [jnp.where(own_first, a, b), jnp.where(own_first, b, a)]
+            a, b = phases[0], other[:, 2 * beams + 1 : 2 * beams + 2]
+            phases = [jnp.where(own_first, a, b), jnp.where(own_first, b, a)]
+        shift = jnp.concatenate(shifts, axis=0).astype(jnp.int32)
+        phase = jnp.concatenate(phases, axis=0)
+        signed = jnp.where(lane >= LANES // 2, lane - LANES, lane) * outer
+        unit = 2.0 * math.pi / (4 * total)
+        coarse = phase - ((signed * shift) & (4 * total - 1)).astype(F32) * unit
+        fine = ((lane * shift) & (4 * total - 1)).astype(F32) * (-unit)
+        tables[level, 0] = jnp.cos(coarse)
+        tables[level, 1] = jnp.sin(coarse)
+        tables[level, 2] = jnp.cos(fine)
+        tables[level, 3] = jnp.sin(fine)
+        if level == final:
+            return
         wide = lax.broadcasted_iota(jnp.int32, (beams, extent), 1)
         mask = (
             lax.broadcasted_iota(jnp.int32, (extent, extent), 0) // beams
@@ -163,43 +190,20 @@
         slot = wide % beams
         second = slot >= half
         place = (slot % half).astype(F32)
-        card_arrival(n // 2).wait_recv()
-        other = cards[(me + n // 2) % n]
-        for level in range(levels):
-            shifts = [column(level, child, half) for child in range(2)]
-            phases = [column(level, 2 + child, half) for child in range(2)]
-            if level == final:
-                own_first = bit(final) == 0
-                a, b = shifts[0], other[:, 2 * beams : 2 * beams + 1]
-                shifts = [jnp.where(own_first, a, b), jnp.where(own_first, b, a)]
-                a, b = phases[0], other[:, 2 * beams + 1 : 2 * beams + 2]
-                phases = [jnp.where(own_first, a, b), jnp.where(own_first, b, a)]
-            shift = jnp.concatenate(shifts, axis=0).astype(jnp.int32)
-            phase = jnp.concatenate(phases, axis=0)
-            signed = jnp.where(lane >= LANES // 2, lane - LANES, lane) * outer
-            unit = 2.0 * math.pi / (4 * total)
-            coarse = phase - ((signed * shift) & (4 * total - 1)).astype(F32) * unit
-            fine = ((lane * shift) & (4 * total - 1)).astype(F32) * (-unit)
-            tables[level, 0] = jnp.cos(coarse)
-            tables[level, 1] = jnp.sin(coarse)
-            tables[level, 2] = jnp.cos(fine)
-            tables[level, 3] = jnp.sin(fine)
-            if level == final:
-                continue
-            first = jnp.where(second, column(level, 5, beams), column(level, 4, beams))
-            block = jnp.zeros((beams, extent), F32)
-            for t in range(taps):
-                weight = jnp.where(second, column(level, 6 + taps + t, beams), column(level, 6 + t, beams))
-                block = block + jnp.where(place == first + t, weight, 0.0)
-            tiled = jnp.concatenate([block] * size, axis=0)
-            high, low = split(jnp.where(mask, tiled, 0.0))
-            merge[level, 0] = high
-            merge[level, 1] = low
+        first = jnp.where(second, column(5, beams), column(4, beams))
+        block = jnp.zeros((beams, extent), F32)
+        for t in range(taps):
+            weight = jnp.where(second, column(6 + taps + t, beams), column(6 + t, beams))
+            block = block + jnp.where(place == first + t, weight, 0.0)
+        tiled = jnp.concatenate([block] * most, axis=0)
+        high, low = split(jnp.where(mask, tiled, 0.0))
+        merge[level, 0] = high
+        merge[level, 1] = low
 
     def level_copy(level, c):
         return pltpu.make_async_remote_copy(
-            src_ref=state.at[level, c, 1 - bit(level)],
-            dst_ref=landed.at[level, c],
+            src_ref=state.at[level, 1 - bit(level), pl.ds(starts[c], sizes[c])],
+            dst_ref=landed.at[level, pl.ds(starts[c], sizes[c])],
             send_sem=level_send.at[level, c],
             recv_sem=level_recv.at[level, c],
             device_id={"sub": across(1 << level)},
@@ -207,9 +211,9 @@
         )
 
     def publish(level, c, values):
-        values = values.reshape(size, 2, half, 2 * LANES)
+        values = values.reshape(sizes[c], 2, half, 2 * LANES)
         for h in range(2):
-            state[level, c, h] = values[:, h]
+            state[level, h, starts[c] : starts[c] + sizes[c]] = values[:, h]
         level_copy(level, c).start()
 
     def transformed(values, w_ref):
@@ -218,40 +222,46 @@
 
     loads[later + 1].wait()
     for c in range(chunks):
-        values = transformed(field[c * size : (c + 1) * size].reshape(size * beams, 2 * LANES), wf_ref)
+        lines = field[starts[c] : starts[c] + sizes[c]].reshape(sizes[c] * beams, 2 * LANES)
+        values = transformed(lines, wf_ref)
         if c == 0:
-            write_card()
             pl.semaphore_wait(barrier, n - 1)
         publish(0, c, values)
+    write_card()
     for v in range(1, n):
         card_copy(v).start()
-    prepare()
+    write_columns()
+    prepare(0)
+    loads[later + 6].wait()
 
     def turned(level, c, both):
         fr, fi = [], []
         cr, ci = tables[level, 0], tables[level, 1]
         sr, si = tables[level, 2], tables[level, 3]
-        for k in range(c * size, (c + 1) * size):
+        for k in range(starts[c], starts[c] + sizes[c]):
             ar, ai = sr[:, k : k + 1], si[:, k : k + 1]
             fr.append(cr * ar - ci * ai)
             fi.append(cr * ai + ci * ar)
         fr, fi = jnp.stack(fr), jnp.stack(fi)
         zr, zi = both[..., :LANES], both[..., LANES:]
-        return jnp.concatenate([zr * fr - zi * fi, zr * fi + zi * fr], axis=-1).reshape(size * beams, 2 * LANES)
+        return jnp.concatenate([zr * fr - zi * fi, zr * fi + zi * fr], axis=-1).reshape(sizes[c] * beams, 2 * LANES)
 
     def stage(level, c):
         level_copy(level, c).wait_recv()
-        kept = state[level, c, bit(level)]
-        both = jnp.concatenate([kept, landed[level, c]], axis=1)
+        size, extent = sizes[c], sizes[c] * beams
+        at = slice(starts[c], starts[c] + size)
+        kept = state[level, bit(level), at]
+        both = jnp.concatenate([kept, landed[level, at]], axis=1)
         high, low = split(turned(level, c, both))
-        values = dot(merge[level, 0], high) + dot(merge[level, 0], low) + dot(merge[level, 1], high)
+        m = [merge[level, i, :extent, :extent] for i in range(2)]
+        values = dot(m[0], high) + dot(m[0], low) + dot(m[1], high)
         if level + 1 < final:
             publish(level + 1, c, values)
             return
         values = turned(final, c, values.reshape(size, beams, 2 * LANES))
         back = transformed(values, wi_ref).reshape(size, beams, 2 * LANES)
         for k in range(size):
-            at = c * size + k
+            at = starts[c] + k
             tr, ti = tw_ref[0, at : at + 1, :], tw_ref[1, at : at + 1, :]
             re, im = back[k, :, :LANES], back[k, :, LANES:]
             field[at, :, :LANES] = re * tr - im * ti
@@ -259,10 +269,17 @@
 
     def turn_order(at):
         level, c = at
-        return (2.1 * level + c if level else c - chunks, level)
-
+        return (2.1 * level * outer / 4 + starts[c] if level else c - chunks, level)
+
+    ready = 1
     for level, c in sorted(((a, b) for a in range(final) for b in range(chunks)), key=turn_order):
+        while ready <= (final if level == final - 1 else level):
+            prepare(ready)
+            ready += 1
         stage(level, c)
+        if level and ready <= final:
+            prepare(ready)
+            ready += 1
 
     for g in range(beams // 8):
         at = slice(g * 8, g * 8 + 8)
@@ -315,34 +332,42 @@
                         moved = pltpu.roll(values, (f - child) * beams % LANES, 1)
                         tiles.append(jnp.where((lane >= f * beams) & (lane < (f + 1) * beams), moved, 0.0))
                 high, low = split(jnp.concatenate(tiles, axis=0))
-                last[h, g, 0] = high
-                last[h, g, 1] = low
+                more[h, g, 0] = high
+                more[h, g, 1] = low
     for level in range(final):
         for c in range(chunks):
             level_copy(level, c).wait_send()
     for v in range(1, n):
         card_copy(v).wait_send()
+    if groups > 1:
+        more[...] = cards[...]
     for v in range(1, n):
         turn_arrival(v).wait_recv()
-    if groups == 1:
-        for r in range(per):
-            for p in range(2):
-                for h in range(2):
-                    for g in range(families):
-                        sides = [
-                            gathered[at : at + 8, r, p, h * half : (h + 1) * half].reshape(LANES // 2, LANES)
-                            for at in (g * 8, n // 2 + g * 8)
-                        ]
-                        high, low = split(jnp.concatenate(sides, axis=0).T)
-                        value = dot(high, last[h, g, 0]) + dot(low, last[h, g, 0]) + dot(high, last[h, g, 1])
-                        at = (h * families + g) * LANES
-                        outs[0][p, r * LANES : (r + 1) * LANES, at : at + LANES] = value
-    else:
+    for v in range(1, n):
+        turn_copy(v).wait_send()
+
+
+def finish(cfg, gathered, last, out_hbm, out_ref, sem):
+    n, per, half = cfg["n"], cfg["per"], cfg["beams"] // 2
+    families = n // 16
+    stores = []
+    for r in range(per):
         for p in range(2):
-            outs[0][:, :, p] = gathered[:, :, p]
-        outs[1][...] = cards[...]
-    for v in range(1, n):
-        turn_copy(v).wait_send()
+            for h in range(2):
+                for g in range(families):
+                    sides = [
+                        gathered[at : at + 8, r, p, h * half : (h + 1) * half].reshape(LANES // 2, LANES)
+                        for at in (g * 8, n // 2 + g * 8)
+                    ]
+                    high, low = split(jnp.concatenate(sides, axis=0).T)
+                    value = dot(high, last[h, g, 0]) + dot(low, last[h, g, 0]) + dot(high, last[h, g, 1])
+                    at = (h * families + g) * LANES
+                    out_ref[p, r * LANES : (r + 1) * LANES, at : at + LANES] = value
+            at = (p, pl.ds(r * LANES, LANES))
+            stores.append(pltpu.make_async_copy(out_ref.at[at], out_hbm.at[at], sem.at[r, p]))
+            stores[-1].start()
+    for store in stores:
+        store.wait()
 
 
 def real_form(length, direction, factor):
@@ -362,16 +387,17 @@
     share = bins // n
     per = max(1, share // LANES)
     groups = max(1, LANES // share)
-    size = CHUNK
-    chunks = outer // size
+    sizes = tuple(part * outer // sum(CHUNKS) for part in CHUNKS)
     rows = beams // groups
-    cfg = dict(n=n, levels=levels, outer=outer, beams=beams, chunks=chunks, per=per, groups=groups,
+    cfg = dict(n=n, levels=levels, outer=outer, beams=beams, sizes=sizes, per=per, groups=groups,
                width=min(share, LANES), rows=rows, taps=taps)
     turns = np.arange(outer)[:, None] * np.arange(LANES)[None, :] * (2.0 * np.pi / bins)
     twiddle = np.stack([np.cos(turns), np.sin(turns)]).astype(np.float32)
     half = beams // 2
-    shapes = [(2, per * LANES, n * beams)] if groups == 1 else [(n, per, 2, rows, LANES), (n, half, LANES)]
-    cfg["outs"] = len(shapes)
+    blocks = -(-levels * (6 + 2 * taps) // LANES)
+    shapes = [((n, per, 2, rows, LANES), F32)]
+    shapes.append(((2, n // 16, 2, LANES, LANES), BF16) if groups == 1 else ((n, half, LANES), F32))
+    held = sum(math.prod(shape) * jnp.dtype(kind).itemsize for shape, kind in shapes)
     vmem = pl.BlockSpec(memory_space=pltpu.VMEM)
     operands = (
         sub_images, shift_table, phase_table, offset_table, weight_table, jnp.asarray(real_form(LANES, -1, 1.0)),
@@ -380,33 +406,41 @@
     result = pl.pallas_call(
         functools.partial(kernel, cfg),
         name="merges",
-        out_shape=[jax.ShapeDtypeStruct(shape, F32) for shape in shapes],
+        out_shape=[pltpu.VMEM(*shape) for shape in shapes],
         in_specs=[pl.BlockSpec(memory_space=pltpu.HBM)] * 8,
         out_specs=[vmem] * len(shapes),
         scratch_shapes=[
             *[pltpu.VMEM(a.shape, a.dtype) for a in operands],
             pltpu.VMEM((outer, beams, 2 * LANES), F32),
-            pltpu.VMEM((levels - 1, chunks, 2, size, beams // 2, 2 * LANES), F32),
-            pltpu.VMEM((levels - 1, chunks, size, beams // 2, 2 * LANES), F32),
-            pltpu.VMEM((-(-levels * (6 + 2 * taps) // LANES) * LANES, LANES), F32),
+            pltpu.VMEM((levels - 1, 2, outer, half, 2 * LANES), F32),
+            pltpu.VMEM((levels - 1, outer, half, 2 * LANES), F32),
+            pltpu.VMEM((blocks * LANES, LANES), F32),
+            pltpu.VMEM((blocks, LANES, LANES), F32),
             pltpu.VMEM((levels, 4, beams, LANES), F32),
-            pltpu.VMEM((levels - 1, 2, size * beams, size * beams), BF16),
-            pltpu.VMEM((n, per, 2, rows, LANES), F32),
+            pltpu.VMEM((levels - 1, 2, max(sizes) * beams, max(sizes) * beams), BF16),
             pltpu.VMEM((n, per, 2, rows, LANES), F32),
             pltpu.VMEM((half, LANES), F32),
             pltpu.VMEM((n, half, LANES), F32),
-            pltpu.VMEM((2, n // 16, 2, LANES, LANES), BF16),
             pltpu.SemaphoreType.DMA((beams // 8 + 7,)),
-            pltpu.SemaphoreType.DMA((levels - 1, chunks)),
-            pltpu.SemaphoreType.DMA((levels - 1, chunks)),
+            pltpu.SemaphoreType.DMA((levels - 1, len(sizes))),
+            pltpu.SemaphoreType.DMA((levels - 1, len(sizes))),
             *[pltpu.SemaphoreType.DMA((n,))] * 4,
         ],
         compiler_params=pltpu.CompilerParams(
-            collective_id=0, has_side_effects=True, vmem_limit_bytes=66400000
+            collective_id=0, has_side_effects=True, vmem_limit_bytes=VMEM - held
         ),
     )(*operands)
     if groups == 1:
-        return result[0]
+        shape = (2, per * LANES, n * beams)
+        return pl.pallas_call(
+            functools.partial(finish, cfg),
+            name="finish",
+            out_shape=jax.ShapeDtypeStruct(shape, F32),
+            in_specs=[vmem] * 2,
+            out_specs=pl.BlockSpec(memory_space=pltpu.HBM),
+            scratch_shapes=[pltpu.VMEM(shape, F32), pltpu.SemaphoreType.DMA((per, 2))],
+            compiler_params=pltpu.CompilerParams(vmem_limit_bytes=24000000),
+        )(*result)
     pieces = result[0].reshape(n, 2, rows, groups, share).transpose(1, 4, 0, 3, 2)
     pieces = pieces.reshape(2, share, 2, n // 2, 2, half)
     blocks = result[1][:, :, : 2 * beams].reshape(2, n // 2, half, 2, beams)

time: 35.8 us -> 32.4 us (0.905)
  the two profiles are of different devices: /device:TPU:11 before, /device:TPU:25 now
where the time goes in v2:
time: 32.4 us; the launch traced here: 32.2 us
  Pallas kernels  32.2 us (99%)
    pallas_call x1, Pallas kernels, body(): pl.pallas_call(functools.partial(kernel, cfg), name='merges', out_shape=[...  31.1 us
    pallas_call x1, Pallas kernels, body(): pl.pallas_call(functools.partial(finish, cfg), name='finish', out_shape=j...  1.14 us

profile of v2, /device:TPU:25, one launch (start us, length us, event | category | flops | bytes accessed | tf_op | source)
XLA Modules:
  0.0 32.2 jit_solution(10326281403251253678)
XLA Ops:
  0.0 31.1 %merges.1 = (f32[16,2,2,16,128]{4,3,2,1,0:T(8,128)S(1)}, bf16[2,1,2,128,128]{4,3,2,1,0:T(8,128)(2,1)S(1)}) custom-call(f32[2,16,4096]{2,1,0:T(8,128)} %x_hbm.1, s32[4,1,2,8]{3,2,1,0:T(2,128)} %shift_hbm.1, f32[4,1,2,8]{3,2,1,0:T(2,128)} %phase_hbm.1, s32[4,1,2,16]{3,2,1,0:T(2,128)} %offset_hbm.1, f32[4,1,2,4,16]{4,3,2,1,0:T(4,128)} %weight_hbm.1, ...), custom_call_target="tpu_custom_call" | custom-call | tf_op jit(solution)/shard_map/merges/pallas_call | solution.py:406
  31.1 1.1 %finish.1 = f32[2,256,256]{2,1,0:T(8,128)} custom-call(f32[16,2,2,16,128]{4,3,2,1,0:T(8,128)S(1)} %get-tuple-element.7.gathered, bf16[2,1,2,128,128]{4,3,2,1,0:T(8,128)(2,1)S(1)} %get-tuple-element.8.last), custom_call_target="tpu_custom_call" | custom-call | tf_op jit(solution)/shard_map/finish/pallas_call | solution.py:435

commit v3 on v2

--- a/solution.py
+++ b/solution.py
@@ -62,8 +62,9 @@
 def kernel(cfg, x_hbm, shift_hbm, phase_hbm, offset_hbm, weight_hbm, wf_hbm, wi_hbm, tw_hbm, *refs):
     gathered, more, refs = refs[0], refs[1], refs[2:]
     (x_ref, shift_ref, phase_ref, offset_ref, weight_ref, wf_ref, wi_ref, tw_ref,
-     field, state, landed, raw, columns, tables, merge, sendbuf, card, cards,
-     load_sem, level_send, level_recv, turn_send, turn_recv, card_send, card_recv) = refs
+     field, state, landed, raw, columns, tables, merge, sendbuf, card, cards, extra, packed,
+     load_sem, level_send, level_recv, turn_send, turn_recv, card_send, card_recv,
+     extra_send, extra_recv, share_send, share_recv) = refs
     n, levels, outer, beams, sizes = cfg["n"], cfg["levels"], cfg["outer"], cfg["beams"], cfg["sizes"]
     per, groups, width, rows = cfg["per"], cfg["groups"], cfg["width"], cfg["rows"]
     half = beams // 2
@@ -76,8 +77,24 @@
     final = levels - 1
     me = lax.axis_index("sub")
 
+    twice = cfg["twice"]
+
+    def bit_of(device, level):
+        return (device // (1 << level)) % 2
+
     def bit(level):
-        return (me // (1 << level)) % 2
+        return bit_of(me, level)
+
+    def inner(device):
+        return (bit_of(device, final) + bit_of(device, final - 1)) % 2 * bit_of(device, 0)
+
+    def facing(device):
+        for level in (final - 1, final):
+            device = device + (1 - 2 * bit_of(device, level)) * (1 << level)
+        return device
+
+    def partial(source, target):
+        return inner(source) * ((bit_of(source, final) + bit_of(target, final)) % 2)
 
     def across(mask):
         other = me
@@ -266,10 +283,23 @@
             re, im = back[k, :, :LANES], back[k, :, LANES:]
             field[at, :, :LANES] = re * tr - im * ti
             field[at, :, LANES:] = im * tr + re * ti
+        if twice:
+
+            @pl.when(inner(me) == 1)
+            def _():
+                extra_copy(c).start()
+
+    def extra_copy(c):
+        at = pl.ds(starts[c], sizes[c])
+        return pltpu.make_async_remote_copy(
+            src_ref=field.at[at, pl.ds(half, half)], dst_ref=extra.at[at],
+            send_sem=extra_send.at[c], recv_sem=extra_recv.at[c],
+            device_id={"sub": facing(me)}, device_id_type=pl.DeviceIdType.MESH,
+        )
 
     def turn_order(at):
         level, c = at
-        return (2.1 * level * outer / 4 + starts[c] if level else c - chunks, level)
+        return (20 * level * outer / 32 + starts[c] if level else c - chunks, level)
 
     ready = 1
     for level, c in sorted(((a, b) for a in range(final) for b in range(chunks)), key=turn_order):
@@ -298,22 +328,68 @@
                     parts = [line[s * rows : (s + 1) * rows, g * width : (g + 1) * width] for s in range(groups)]
                     sendbuf[q * groups + g, 0, p] = jnp.concatenate(parts, axis=1)
 
-    def turn_copy(v):
-        there = (me + v) % n
+    def turn_copy(v, source, lines):
+        target = (source + v) % n
+        here = target if source is me else source
         return pltpu.make_async_remote_copy(
-            src_ref=sendbuf.at[there], dst_ref=gathered.at[me], send_sem=turn_send.at[v], recv_sem=turn_recv.at[v],
-            device_id={"sub": there}, device_id_type=pl.DeviceIdType.MESH,
-        )
-
-    def turn_arrival(v):
-        here = (me + n - v) % n
+            src_ref=sendbuf.at[here, :, :, pl.ds(0, lines)], dst_ref=gathered.at[source, :, :, pl.ds(0, lines)],
+            send_sem=turn_send.at[v], recv_sem=turn_recv.at[v],
+            device_id={"sub": here}, device_id_type=pl.DeviceIdType.MESH,
+        )
+
+    def each_turn(v, arrives, act):
+        source = (me + n - v) % n if arrives else me
+        if not twice:
+            act(turn_copy(v, source, rows))
+            return
+        part = partial(source, (source + v) % n)
+
+        @pl.when(part == 0)
+        def _():
+            act(turn_copy(v, source, rows))
+
+        @pl.when(part == 1)
+        def _():
+            act(turn_copy(v, source, half))
+
+    def share_copy(slot, source, target):
         return pltpu.make_async_remote_copy(
-            src_ref=sendbuf.at[here], dst_ref=gathered.at[here], send_sem=turn_send.at[v], recv_sem=turn_recv.at[v],
-            device_id={"sub": here}, device_id_type=pl.DeviceIdType.MESH,
-        )
+            src_ref=packed.at[slot], dst_ref=gathered.at[facing(source), :, :, pl.ds(half, half)],
+            send_sem=share_send.at[slot], recv_sem=share_recv.at[source % (n // 2)],
+            device_id={"sub": target}, device_id_type=pl.DeviceIdType.MESH,
+        )
+
+    def each_share(act):
+        for slot in range(n // 2):
+            target = bit(final) * (n // 2) + slot
+
+            @pl.when(inner(me) * jnp.where(target == me, 0, 1) == 1)
+            def _():
+                act(share_copy(slot, me, target))
 
     for v in range(1, n):
-        turn_copy(v).start()
+        each_turn(v, False, lambda copy: copy.start())
+    if twice:
+
+        @pl.when(inner(me) == 1)
+        def _():
+            for c in range(chunks):
+                extra_copy(c).wait_recv()
+            lines = [(extra[k, :, :LANES], extra[k, :, LANES:]) for k in range(outer)]
+            even, odd = butterflies(lines[0::2], 1), butterflies(lines[1::2], 1)
+            sign = (1 - 2 * bit(final)).astype(F32)
+            for k in range(outer // 2):
+                angle = 2.0 * math.pi * k / outer
+                turn = times_constant(odd[k], complex(math.cos(angle), math.sin(angle)))
+                for p in range(2):
+                    packed[k // per, k % per, p] = even[k][p] + sign * turn[p]
+
+        each_share(lambda copy: copy.start())
+
+        @pl.when(inner(me) == 1)
+        def _():
+            gathered[facing(me), :, :, half:] = packed[me % (n // 2)]
+
     gathered[me] = sendbuf[me]
     cards[me] = card[...]
     for v in range(1, n):
@@ -342,9 +418,23 @@
     if groups > 1:
         more[...] = cards[...]
     for v in range(1, n):
-        turn_arrival(v).wait_recv()
+        each_turn(v, True, lambda copy: copy.wait_recv())
+    if twice:
+        for slot in range(n // 2):
+            source = bit(final) * (n // 2) + slot
+
+            @pl.when(inner(source) * jnp.where(source == me, 0, 1) == 1)
+            def _():
+                share_copy(slot, source, source).wait_recv()
     for v in range(1, n):
-        turn_copy(v).wait_send()
+        each_turn(v, False, lambda copy: copy.wait_send())
+    if twice:
+        each_share(lambda copy: copy.wait_send())
+
+        @pl.when(inner(me) == 1)
+        def _():
+            for c in range(chunks):
+                extra_copy(c).wait_send()
 
 
 def finish(cfg, gathered, last, out_hbm, out_ref, sem):
@@ -390,7 +480,7 @@
     sizes = tuple(part * outer // sum(CHUNKS) for part in CHUNKS)
     rows = beams // groups
     cfg = dict(n=n, levels=levels, outer=outer, beams=beams, sizes=sizes, per=per, groups=groups,
-               width=min(share, LANES), rows=rows, taps=taps)
+               width=min(share, LANES), rows=rows, taps=taps, twice=groups == 1 and levels > 2)
     turns = np.arange(outer)[:, None] * np.arange(LANES)[None, :] * (2.0 * np.pi / bins)
     twiddle = np.stack([np.cos(turns), np.sin(turns)]).astype(np.float32)
     half = beams // 2
@@ -421,10 +511,14 @@
             pltpu.VMEM((n, per, 2, rows, LANES), F32),
             pltpu.VMEM((half, LANES), F32),
             pltpu.VMEM((n, half, LANES), F32),
+            pltpu.VMEM((outer, half, 2 * LANES), F32),
+            pltpu.VMEM((n // 2, per, 2, half, LANES), F32),
             pltpu.SemaphoreType.DMA((beams // 8 + 7,)),
             pltpu.SemaphoreType.DMA((levels - 1, len(sizes))),
             pltpu.SemaphoreType.DMA((levels - 1, len(sizes))),
             *[pltpu.SemaphoreType.DMA((n,))] * 4,
+            *[pltpu.SemaphoreType.DMA((len(sizes),))] * 2,
+            *[pltpu.SemaphoreType.DMA((n // 2,))] * 2,
         ],
         compiler_params=pltpu.CompilerParams(
             collective_id=0, has_side_effects=True, vmem_limit_bytes=VMEM - held

time: 32.4 us -> 31.5 us (0.972)
  the two profiles are of different devices: /device:TPU:25 before, /device:TPU:0 now
where the time goes in v3:
time: 31.5 us; the launch traced here: 31.3 us
  Pallas kernels  31.3 us (99%)
    pallas_call x1, Pallas kernels, body(): pl.pallas_call(functools.partial(kernel, cfg), name='merges', out_shape=[...  30.1 us
    pallas_call x1, Pallas kernels, body(): pl.pallas_call(functools.partial(finish, cfg), name='finish', out_shape=j...  1.14 us

profile of v3, /device:TPU:0, one launch (start us, length us, event | category | flops | bytes accessed | tf_op | source)
XLA Modules:
  0.0 31.3 jit_solution(5628813621126898566)
XLA Ops:
  0.0 30.1 %merges.1 = (f32[16,2,2,16,128]{4,3,2,1,0:T(8,128)S(1)}, bf16[2,1,2,128,128]{4,3,2,1,0:T(8,128)(2,1)S(1)}) custom-call(f32[2,16,4096]{2,1,0:T(8,128)} %x_hbm.1, s32[4,1,2,8]{3,2,1,0:T(2,128)} %shift_hbm.1, f32[4,1,2,8]{3,2,1,0:T(2,128)} %phase_hbm.1, s32[4,1,2,16]{3,2,1,0:T(2,128)} %offset_hbm.1, f32[4,1,2,4,16]{4,3,2,1,0:T(4,128)} %weight_hbm.1, ...), custom_call_target="tpu_custom_call" | custom-call | tf_op jit(solution)/shard_map/merges/pallas_call | solution.py:496
  30.2 1.1 %finish.1 = f32[2,256,256]{2,1,0:T(8,128)} custom-call(f32[16,2,2,16,128]{4,3,2,1,0:T(8,128)S(1)} %get-tuple-element.7.gathered, bf16[2,1,2,128,128]{4,3,2,1,0:T(8,128)(2,1)S(1)} %get-tuple-element.8.last), custom_call_target="tpu_custom_call" | custom-call | tf_op jit(solution)/shard_map/finish/pallas_call | solution.py:529

commit v4 on v3

--- a/solution.py
+++ b/solution.py
@@ -10,7 +10,9 @@
 from jax.sharding import PartitionSpec as P
 
 LANES = 128
-CHUNKS = (1, 1, 2, 2, 1, 1)
+CHUNKS = (1, 2, 2, 1, 1, 1)
+AHEAD = 3
+GAP = 20
 VMEM = 67043328 - (3 << 16)
 F32 = jnp.float32
 BF16 = jnp.bfloat16
@@ -63,8 +65,10 @@
     gathered, more, refs = refs[0], refs[1], refs[2:]
     (x_ref, shift_ref, phase_ref, offset_ref, weight_ref, wf_ref, wi_ref, tw_ref,
      field, state, landed, raw, columns, tables, merge, sendbuf, card, cards, extra, packed,
-     load_sem, level_send, level_recv, turn_send, turn_recv, card_send, card_recv,
-     extra_send, extra_recv, share_send, share_recv) = refs
+     load_sem, level_send, level_recv, pooled) = refs
+    turn_send, turn_recv, card_send, card_recv, facing_recv, extra_send, extra_recv, share_send, share_recv = (
+        pooled.at[i] for i in range(9)
+    )
     n, levels, outer, beams, sizes = cfg["n"], cfg["levels"], cfg["outer"], cfg["beams"], cfg["sizes"]
     per, groups, width, rows = cfg["per"], cfg["groups"], cfg["width"], cfg["rows"]
     half = beams // 2
@@ -92,9 +96,6 @@
         for level in (final - 1, final):
             device = device + (1 - 2 * bit_of(device, level)) * (1 << level)
         return device
-
-    def partial(source, target):
-        return inner(source) * ((bit_of(source, final) + bit_of(target, final)) % 2)
 
     def across(mask):
         other = me
@@ -127,22 +128,20 @@
             field[k, g * 8 : g * 8 + 8, :LANES] = re * tr + im * ti
             field[k, g * 8 : g * 8 + 8, LANES:] = im * tr - re * ti
 
+    def all_of(source, target, send, recv):
+        return pltpu.make_async_remote_copy(
+            src_ref=source, dst_ref=target, send_sem=send, recv_sem=recv,
+            device_id={"sub": across(1)}, device_id_type=pl.DeviceIdType.MESH,
+        )
+
     def card_copy(v):
         there = (me + v) % n
         return pltpu.make_async_remote_copy(
-            src_ref=card, dst_ref=cards.at[me], send_sem=card_send.at[v], recv_sem=card_recv.at[v],
+            src_ref=card, dst_ref=cards.at[me], send_sem=card_send, recv_sem=facing_recv if v == n // 2 else card_recv,
             device_id={"sub": there}, device_id_type=pl.DeviceIdType.MESH,
         )
 
-    def card_arrival(v):
-        return pltpu.make_async_remote_copy(
-            src_ref=card, dst_ref=cards.at[(me + n - v) % n], send_sem=card_send.at[v], recv_sem=card_recv.at[v],
-            device_id={"sub": (me + n - v) % n}, device_id_type=pl.DeviceIdType.MESH,
-        )
-
     def write_card():
-        for load in loads[later + 2 : later + 6]:
-            load.wait()
         place = lax.broadcasted_iota(jnp.int32, (half, beams), 0)
         blocks = []
         for child in range(2):
@@ -180,8 +179,9 @@
         shifts = [column(child, half) for child in range(2)]
         phases = [column(2 + child, half) for child in range(2)]
         if level == final:
-            card_arrival(n // 2).wait_recv()
-            other = cards[(me + n // 2) % n]
+            opposite = (me + n // 2) % n
+            all_of(card, cards.at[opposite], card_send, facing_recv).wait_recv()
+            other = cards[opposite]
             own_first = bit(final) == 0
             a, b = shifts[0], other[:, 2 * beams : 2 * beams + 1]
             shifts = [jnp.where(own_first, a, b), jnp.where(own_first, b, a)]
@@ -221,7 +221,7 @@
         return pltpu.make_async_remote_copy(
             src_ref=state.at[level, 1 - bit(level), pl.ds(starts[c], sizes[c])],
             dst_ref=landed.at[level, pl.ds(starts[c], sizes[c])],
-            send_sem=level_send.at[level, c],
+            send_sem=level_send.at[level],
             recv_sem=level_recv.at[level, c],
             device_id={"sub": across(1 << level)},
             device_id_type=pl.DeviceIdType.MESH,
@@ -236,20 +236,6 @@
     def transformed(values, w_ref):
         high, low = split(values)
         return dot(high, w_ref[0]) + dot(low, w_ref[0]) + dot(high, w_ref[1])
-
-    loads[later + 1].wait()
-    for c in range(chunks):
-        lines = field[starts[c] : starts[c] + sizes[c]].reshape(sizes[c] * beams, 2 * LANES)
-        values = transformed(lines, wf_ref)
-        if c == 0:
-            pl.semaphore_wait(barrier, n - 1)
-        publish(0, c, values)
-    write_card()
-    for v in range(1, n):
-        card_copy(v).start()
-    write_columns()
-    prepare(0)
-    loads[later + 6].wait()
 
     def turned(level, c, both):
         fr, fi = [], []
@@ -293,21 +279,43 @@
         at = pl.ds(starts[c], sizes[c])
         return pltpu.make_async_remote_copy(
             src_ref=field.at[at, pl.ds(half, half)], dst_ref=extra.at[at],
-            send_sem=extra_send.at[c], recv_sem=extra_recv.at[c],
+            send_sem=extra_send, recv_sem=extra_recv,
             device_id={"sub": facing(me)}, device_id_type=pl.DeviceIdType.MESH,
         )
 
     def turn_order(at):
         level, c = at
-        return (20 * level * outer / 32 + starts[c] if level else c - chunks, level)
-
+        return (GAP * level * outer / 32 + starts[c], level)
+
+    def spectrum(c):
+        lines = field[starts[c] : starts[c] + sizes[c]].reshape(sizes[c] * beams, 2 * LANES)
+        values = transformed(lines, wf_ref)
+        if c == 0:
+            pl.semaphore_wait(barrier, n - 1)
+        publish(0, c, values)
+
+    loads[later + 1].wait()
+    for c in range(AHEAD):
+        spectrum(c)
+    for load in loads[later + 2 : later + 6]:
+        load.wait()
+    write_card()
+    for v in range(1, n):
+        card_copy(v).start()
+    write_columns()
+    prepare(0)
+    for c in range(chunks):
+        stage(0, c)
+        if c + AHEAD < chunks:
+            spectrum(c + AHEAD)
+    loads[later + 6].wait()
     ready = 1
-    for level, c in sorted(((a, b) for a in range(final) for b in range(chunks)), key=turn_order):
+    for level, c in sorted(((a, b) for a in range(1, final) for b in range(chunks)), key=turn_order):
         while ready <= (final if level == final - 1 else level):
             prepare(ready)
             ready += 1
         stage(level, c)
-        if level and ready <= final:
+        if ready < final:
             prepare(ready)
             ready += 1
 
@@ -328,53 +336,41 @@
                     parts = [line[s * rows : (s + 1) * rows, g * width : (g + 1) * width] for s in range(groups)]
                     sendbuf[q * groups + g, 0, p] = jnp.concatenate(parts, axis=1)
 
-    def turn_copy(v, source, lines):
-        target = (source + v) % n
-        here = target if source is me else source
+    def turn_send_to(there, rows):
+        lines = pl.ds(0, rows)
+        pltpu.make_async_remote_copy(
+            src_ref=sendbuf.at[there, :, :, lines], dst_ref=gathered.at[me, :, :, lines],
+            send_sem=turn_send, recv_sem=turn_recv,
+            device_id={"sub": there}, device_id_type=pl.DeviceIdType.MESH,
+        ).start()
+
+    for v in range(1, n):
+        there = (me + v) % n
+        if not twice:
+            turn_send_to(there, rows)
+            continue
+        part = inner(me) * ((bit(final) + bit_of(there, final)) % 2)
+        pl.when(part == 0)(functools.partial(turn_send_to, there, rows))
+        pl.when(part == 1)(functools.partial(turn_send_to, there, half))
+
+    def share_copy(slot, target):
         return pltpu.make_async_remote_copy(
-            src_ref=sendbuf.at[here, :, :, pl.ds(0, lines)], dst_ref=gathered.at[source, :, :, pl.ds(0, lines)],
-            send_sem=turn_send.at[v], recv_sem=turn_recv.at[v],
-            device_id={"sub": here}, device_id_type=pl.DeviceIdType.MESH,
-        )
-
-    def each_turn(v, arrives, act):
-        source = (me + n - v) % n if arrives else me
-        if not twice:
-            act(turn_copy(v, source, rows))
-            return
-        part = partial(source, (source + v) % n)
-
-        @pl.when(part == 0)
-        def _():
-            act(turn_copy(v, source, rows))
-
-        @pl.when(part == 1)
-        def _():
-            act(turn_copy(v, source, half))
-
-    def share_copy(slot, source, target):
-        return pltpu.make_async_remote_copy(
-            src_ref=packed.at[slot], dst_ref=gathered.at[facing(source), :, :, pl.ds(half, half)],
-            send_sem=share_send.at[slot], recv_sem=share_recv.at[source % (n // 2)],
+            src_ref=packed.at[slot], dst_ref=gathered.at[facing(me), :, :, pl.ds(half, half)],
+            send_sem=share_send, recv_sem=share_recv,
             device_id={"sub": target}, device_id_type=pl.DeviceIdType.MESH,
         )
 
-    def each_share(act):
-        for slot in range(n // 2):
-            target = bit(final) * (n // 2) + slot
-
-            @pl.when(inner(me) * jnp.where(target == me, 0, 1) == 1)
-            def _():
-                act(share_copy(slot, me, target))
-
-    for v in range(1, n):
-        each_turn(v, False, lambda copy: copy.start())
+    def shared(count):
+        return all_of(packed.at[pl.ds(0, count)], packed.at[pl.ds(0, count)], share_send, share_recv)
+
+    def turned_slabs(count):
+        return all_of(sendbuf.at[pl.ds(0, count)], gathered.at[pl.ds(0, count)], turn_send, turn_recv)
+
     if twice:
 
         @pl.when(inner(me) == 1)
         def _():
-            for c in range(chunks):
-                extra_copy(c).wait_recv()
+            all_of(extra, extra, extra_send, extra_recv).wait_recv()
             lines = [(extra[k, :, :LANES], extra[k, :, LANES:]) for k in range(outer)]
             even, odd = butterflies(lines[0::2], 1), butterflies(lines[1::2], 1)
             sign = (1 - 2 * bit(final)).astype(F32)
@@ -384,7 +380,9 @@
                 for p in range(2):
                     packed[k // per, k % per, p] = even[k][p] + sign * turn[p]
 
-        each_share(lambda copy: copy.start())
+        for slot in range(n // 2):
+            target = bit(final) * (n // 2) + slot
+            pl.when(inner(me) * jnp.where(target == me, 0, 1) == 1)(share_copy(slot, target).start)
 
         @pl.when(inner(me) == 1)
         def _():
@@ -392,9 +390,7 @@
 
     gathered[me] = sendbuf[me]
     cards[me] = card[...]
-    for v in range(1, n):
-        if v != n // 2:
-            card_arrival(v).wait_recv()
+    all_of(cards.at[pl.ds(0, n - 2)], cards.at[pl.ds(0, n - 2)], card_send, card_recv).wait_recv()
     families = n // 16
     if groups == 1:
         lane = lax.broadcasted_iota(jnp.int32, (half, LANES), 1)
@@ -411,30 +407,28 @@
                 more[h, g, 0] = high
                 more[h, g, 1] = low
     for level in range(final):
-        for c in range(chunks):
-            level_copy(level, c).wait_send()
-    for v in range(1, n):
-        card_copy(v).wait_send()
+        sent = state.at[level, 1 - bit(level)]
+        all_of(sent, landed.at[level], level_send.at[level], level_recv.at[level, 0]).wait_send()
+    all_of(cards.at[pl.ds(0, n - 1)], cards.at[pl.ds(0, n - 1)], card_send, card_recv).wait_send()
     if groups > 1:
         more[...] = cards[...]
-    for v in range(1, n):
-        each_turn(v, True, lambda copy: copy.wait_recv())
-    if twice:
-        for slot in range(n // 2):
-            source = bit(final) * (n // 2) + slot
-
-            @pl.when(inner(source) * jnp.where(source == me, 0, 1) == 1)
-            def _():
-                share_copy(slot, source, source).wait_recv()
-    for v in range(1, n):
-        each_turn(v, False, lambda copy: copy.wait_send())
-    if twice:
-        each_share(lambda copy: copy.wait_send())
-
-        @pl.when(inner(me) == 1)
-        def _():
-            for c in range(chunks):
-                extra_copy(c).wait_send()
+    if not twice:
+        turned_slabs(n - 1).wait_recv()
+        turned_slabs(n - 1).wait_send()
+        return
+    turned_slabs(n - 1 - n // 16).wait_recv()
+
+    @pl.when(inner(me) == 0)
+    def _():
+        shared(n // 8).wait_recv()
+        turned_slabs(n - 1).wait_send()
+
+    @pl.when(inner(me) == 1)
+    def _():
+        shared(n // 8 - 1).wait_recv()
+        turned_slabs(n - 1 - n // 4).wait_send()
+        shared(n // 2 - 1).wait_send()
+        all_of(extra, extra, extra_send, extra_recv).wait_send()
 
 
 def finish(cfg, gathered, last, out_hbm, out_ref, sem):
@@ -514,11 +508,9 @@
             pltpu.VMEM((outer, half, 2 * LANES), F32),
             pltpu.VMEM((n // 2, per, 2, half, LANES), F32),
             pltpu.SemaphoreType.DMA((beams // 8 + 7,)),
+            pltpu.SemaphoreType.DMA((levels - 1,)),
             pltpu.SemaphoreType.DMA((levels - 1, len(sizes))),
-            pltpu.SemaphoreType.DMA((levels - 1, len(sizes))),
-            *[pltpu.SemaphoreType.DMA((n,))] * 4,
-            *[pltpu.SemaphoreType.DMA((len(sizes),))] * 2,
-            *[pltpu.SemaphoreType.DMA((n // 2,))] * 2,
+            pltpu.SemaphoreType.DMA((9,)),
         ],
         compiler_params=pltpu.CompilerParams(
             collective_id=0, has_side_effects=True, vmem_limit_bytes=VMEM - held

time: 31.5 us -> 29.8 us (0.946)
  Pallas kernels: 31.3 us -> 29.6 us
    pallas_call x1, Pallas kernels: 30.1 us -> 28.4 us  [body(): pl.pallas_call(functools.partial(kernel, cfg), name='merges', out_shape=[...]
where the time goes in v4:
time: 29.8 us; the launch traced here: 29.6 us
  Pallas kernels  29.6 us (99%)
    pallas_call x1, Pallas kernels, body(): pl.pallas_call(functools.partial(kernel, cfg), name='merges', out_shape=[...  28.4 us
    pallas_call x1, Pallas kernels, body(): pl.pallas_call(functools.partial(finish, cfg), name='finish', out_shape=j...  1.13 us

profile of v4, /device:TPU:0, one launch (start us, length us, event | category | flops | bytes accessed | tf_op | source)
XLA Modules:
  0.0 29.6 jit_solution(8103749843348401220)
XLA Ops:
  0.0 28.4 %merges.1 = (f32[16,2,2,16,128]{4,3,2,1,0:T(8,128)S(1)}, bf16[2,1,2,128,128]{4,3,2,1,0:T(8,128)(2,1)S(1)}) custom-call(f32[2,16,4096]{2,1,0:T(8,128)} %x_hbm.1, s32[4,1,2,8]{3,2,1,0:T(2,128)} %shift_hbm.1, f32[4,1,2,8]{3,2,1,0:T(2,128)} %phase_hbm.1, s32[4,1,2,16]{3,2,1,0:T(2,128)} %offset_hbm.1, f32[4,1,2,4,16]{4,3,2,1,0:T(4,128)} %weight_hbm.1, ...), custom_call_target="tpu_custom_call" | custom-call | tf_op jit(solution)/shard_map/merges/pallas_call | solution.py:490
  28.4 1.1 %finish.1 = f32[2,256,256]{2,1,0:T(8,128)} custom-call(f32[16,2,2,16,128]{4,3,2,1,0:T(8,128)S(1)} %get-tuple-element.7.gathered, bf16[2,1,2,128,128]{4,3,2,1,0:T(8,128)(2,1)S(1)} %get-tuple-element.8.last), custom_call_target="tpu_custom_call" | custom-call | tf_op jit(solution)/shard_map/finish/pallas_call | solution.py:521

commit v5 on v4

--- a/solution.py
+++ b/solution.py
@@ -12,7 +12,8 @@
 LANES = 128
 CHUNKS = (1, 2, 2, 1, 1, 1)
 AHEAD = 3
-GAP = 20
+GAP = 26
+TOGETHER = 2
 VMEM = 67043328 - (3 << 16)
 F32 = jnp.float32
 BF16 = jnp.bfloat16
@@ -435,8 +436,10 @@
     n, per, half = cfg["n"], cfg["per"], cfg["beams"] // 2
     families = n // 16
     stores = []
-    for r in range(per):
-        for p in range(2):
+    tiles = [(r, p) for r in range(per) for p in range(2)]
+    for first in range(0, len(tiles), TOGETHER):
+        group = tiles[first : first + TOGETHER]
+        for r, p in group:
             for h in range(2):
                 for g in range(families):
                     sides = [
@@ -447,6 +450,7 @@
                     value = dot(high, last[h, g, 0]) + dot(low, last[h, g, 0]) + dot(high, last[h, g, 1])
                     at = (h * families + g) * LANES
                     out_ref[p, r * LANES : (r + 1) * LANES, at : at + LANES] = value
+        for r, p in group:
             at = (p, pl.ds(r * LANES, LANES))
             stores.append(pltpu.make_async_copy(out_ref.at[at], out_hbm.at[at], sem.at[r, p]))
             stores[-1].start()

time: 29.8 us -> 29.8 us (level)
  no operation moved by 1% of the time
where the time goes in v5:
time: 29.8 us; the launch traced here: 29.7 us
  Pallas kernels  29.7 us (100%)
    pallas_call x1, Pallas kernels, body(): pl.pallas_call(functools.partial(kernel, cfg), name='merges', out_shape=[...  28.5 us
    pallas_call x1, Pallas kernels, body(): pl.pallas_call(functools.partial(finish, cfg), name='finish', out_shape=j...  1.18 us

profile of v5, /device:TPU:0, one launch (start us, length us, event | category | flops | bytes accessed | tf_op | source)
XLA Modules:
  0.0 29.7 jit_solution(16586965308874553340)
XLA Ops:
  0.0 28.5 %merges.1 = (f32[16,2,2,16,128]{4,3,2,1,0:T(8,128)S(1)}, bf16[2,1,2,128,128]{4,3,2,1,0:T(8,128)(2,1)S(1)}) custom-call(f32[2,16,4096]{2,1,0:T(8,128)} %x_hbm.1, s32[4,1,2,8]{3,2,1,0:T(2,128)} %shift_hbm.1, f32[4,1,2,8]{3,2,1,0:T(2,128)} %phase_hbm.1, s32[4,1,2,16]{3,2,1,0:T(2,128)} %offset_hbm.1, f32[4,1,2,4,16]{4,3,2,1,0:T(4,128)} %weight_hbm.1, ...), custom_call_target="tpu_custom_call" | custom-call | tf_op jit(solution)/shard_map/merges/pallas_call | solution.py:494
  28.5 1.2 %finish.1 = f32[2,256,256]{2,1,0:T(8,128)} custom-call(f32[16,2,2,16,128]{4,3,2,1,0:T(8,128)S(1)} %get-tuple-element.7.gathered, bf16[2,1,2,128,128]{4,3,2,1,0:T(8,128)(2,1)S(1)} %get-tuple-element.8.last), custom_call_target="tpu_custom_call" | custom-call | tf_op jit(solution)/shard_map/finish/pallas_call | solution.py:525

commit v6 on v4

--- a/solution.py
+++ b/solution.py
@@ -10,9 +10,9 @@
 from jax.sharding import PartitionSpec as P
 
 LANES = 128
-CHUNKS = (1, 2, 2, 1, 1, 1)
+CHUNKS = (1, 1, 1, 2, 1, 1, 1)
 AHEAD = 3
-GAP = 20
+GAP = 26
 VMEM = 67043328 - (3 << 16)
 F32 = jnp.float32
 BF16 = jnp.bfloat16

time: 29.8 us -> 29.7 us (level)
  no operation moved by 1% of the time
where the time goes in v6:
time: 29.7 us; the launch traced here: 29.5 us
  Pallas kernels  29.5 us (99%)
    pallas_call x1, Pallas kernels, body(): pl.pallas_call(functools.partial(kernel, cfg), name='merges', out_shape=[...  28.4 us
    pallas_call x1, Pallas kernels, body(): pl.pallas_call(functools.partial(finish, cfg), name='finish', out_shape=j...  1.13 us

profile of v6, /device:TPU:0, one launch (start us, length us, event | category | flops | bytes accessed | tf_op | source)
XLA Modules:
  0.0 29.5 jit_solution(13014173767148275595)
XLA Ops:
  0.0 28.4 %merges.1 = (f32[16,2,2,16,128]{4,3,2,1,0:T(8,128)S(1)}, bf16[2,1,2,128,128]{4,3,2,1,0:T(8,128)(2,1)S(1)}) custom-call(f32[2,16,4096]{2,1,0:T(8,128)} %x_hbm.1, s32[4,1,2,8]{3,2,1,0:T(2,128)} %shift_hbm.1, f32[4,1,2,8]{3,2,1,0:T(2,128)} %phase_hbm.1, s32[4,1,2,16]{3,2,1,0:T(2,128)} %offset_hbm.1, f32[4,1,2,4,16]{4,3,2,1,0:T(4,128)} %weight_hbm.1, ...), custom_call_target="tpu_custom_call" | custom-call | tf_op jit(solution)/shard_map/merges/pallas_call | solution.py:490
  28.4 1.1 %finish.1 = f32[2,256,256]{2,1,0:T(8,128)} custom-call(f32[16,2,2,16,128]{4,3,2,1,0:T(8,128)S(1)} %get-tuple-element.7.gathered, bf16[2,1,2,128,128]{4,3,2,1,0:T(8,128)(2,1)S(1)} %get-tuple-element.8.last), custom_call_target="tpu_custom_call" | custom-call | tf_op jit(solution)/shard_map/finish/pallas_call | solution.py:521
